TPU v7x, 256 devices: a whole 4x4x8 slice. The times are simulated.
256 devices in a mesh: leaf: 16 (over y, x), blk: 16 (over z, core).
Axes of the slice: x: 4, y: 4, z: 8, core: 2. Of those that a mesh axis runs over, the one named last changes fastest.
Arguments:
- leaf_rhs: bfloat16 [81920, 256], P(('leaf', 'blk')), may hold values from -6 to 6
- leaf_inverse: bfloat16 [81920, 5120], P(('leaf', 'blk')), may hold values from -0.078125 to 0.078125
- leaf_lower: bfloat16 [32768, 5120], P(('leaf', 'blk')), may hold values from -0.078125 to 0.078125
- sep_rhs: bfloat16 [4, 16384, 256], P(None, ('leaf', 'blk')), may hold values from -6 to 6
- sep_inverse: bfloat16 [16384, 30720], P(('leaf', 'blk'))
- sep_lower: bfloat16 [32768, 14336], P(('leaf', 'blk'))
- slot_map: int32 [4, 256, 2], P(None, ('leaf', 'blk')), may hold values from 0 to 5, as said below
Outputs:
- leaf_solution: bfloat16 [81920, 256], P(('leaf', 'blk'))
- sep_solution: bfloat16 [4, 16384, 256], P(None, ('leaf', 'blk'))
Inputs may be any that keep to these rules, and one draw needn't show every extreme that they name: For every level below the top, slot_map[h-1, q] holds two different numbers of 0 to 5; at the top level it holds 0 and 1 in some order.
All inputs are finite; a program needn't handle non-finite values.
Results may differ from a plain program's by a relative error of at most 0.015.
Values may be sent and summed in bfloat16 or wider, within the bound.
A program may use at most 128 MiB of HBM per device.

v0:
```python
import jax
import jax.numpy as jnp
from jax import lax
from jax.sharding import PartitionSpec as P


def partner(value, axis, apart):
    mask = 2**apart
    pairs = [(source, source ^ mask) for source in range(lax.axis_size(axis))]
    return lax.ppermute(value, axis, pairs)


def from_everyone(shard, axis):
    length = lax.axis_size(axis)
    return lax.all_to_all(
        jnp.broadcast_to(shard[None], (length, *shard.shape)), axis, 0, 0, tiled=True
    )


def laid_out(blocks, dim):
    blocks = jnp.moveaxis(blocks, 0, dim)
    shape = blocks.shape
    return blocks.reshape(*shape[:dim], shape[dim] * shape[dim + 1], *shape[dim + 2 :])


def gather_directly(shard, axis, dim):
    blocks = from_everyone(shard, axis)
    return laid_out(blocks, dim)


def pair_merge(mine, partner_rows, bit_index):
    upper_bit = jnp.bitwise_and(jnp.right_shift(lax.axis_index("leaf"), bit_index), 1)
    lower_half = jnp.where(upper_bit == 1, partner_rows, mine)
    upper_half = jnp.where(upper_bit == 1, mine, partner_rows)
    return jnp.concatenate([lower_half, upper_half], axis=0)


def group_rows(pieces, height):
    joined = pieces
    for bit_index in range(height):
        partner_rows = partner(joined, "leaf", bit_index)
        joined = pair_merge(joined, partner_rows, bit_index)
    spread = lax.all_gather(joined, "blk", axis=0, tiled=True)
    spread = spread.reshape(lax.axis_size("blk"), 2**height, pieces.shape[0], pieces.shape[1])
    return jnp.transpose(spread, (1, 0, 2, 3)).reshape(-1, pieces.shape[1])


def on_device(leaf_rhs, leaf_inverse, leaf_lower, sep_rhs, sep_inverse, sep_lower, slot_map):
    columns = leaf_rhs.shape[1]
    levels = sep_rhs.shape[0]
    pivots = sep_rhs.shape[1]
    base_width = pivots * lax.axis_size("blk")
    section = leaf_inverse
    leaf_solution = jnp.dot(
        section, gather_directly(leaf_rhs, "blk", 0), preferred_element_type=jnp.float32
    ).astype(jnp.bfloat16)
    section = leaf_lower
    update = -jnp.dot(
        section, gather_directly(leaf_solution, "blk", 0), preferred_element_type=jnp.float32
    )
    solutions = []
    for height in range(1, levels + 1):
        at_root = height == levels
        front_slots = 1 if at_root else 3
        slot_rows = update.reshape(2, pivots, columns)
        onehot = (
            slot_map[height - 1, 0][:, None]
            == jnp.arange(2 * front_slots, dtype=jnp.int32)[None, :]
        ).astype(jnp.float32)
        mixed = jnp.einsum("st,spr->tpr", onehot, slot_rows, precision=lax.Precision.HIGHEST)
        received = partner(mixed[front_slots:].astype(jnp.bfloat16), "leaf", height - 1).astype(
            jnp.float32
        )
        front_rows = mixed[:front_slots] + received
        pivot_front = (sep_rhs[height - 1].astype(jnp.float32) + front_rows[0]).astype(jnp.bfloat16)
        width_now = base_width * 2**height
        offset = base_width * (2**height - 2)
        gathered = group_rows(pivot_front, height)
        solved = jnp.dot(
            sep_inverse[:, offset : offset + width_now],
            gathered,
            preferred_element_type=jnp.float32,
        ).astype(jnp.bfloat16)
        solutions.append(solved)
        if not at_root:
            spread = group_rows(solved, height)
            product = jnp.dot(
                sep_lower[:, offset : offset + width_now],
                spread,
                preferred_element_type=jnp.float32,
            )
            update = front_rows[1:].reshape(2 * pivots, columns) - product
    return (leaf_solution, jnp.stack(solutions))


def solution(mesh):
    return jax.shard_map(
        on_device,
        mesh=mesh,
        in_specs=(
            P(("leaf", "blk"), None),
            P(("leaf", "blk"), None),
            P(("leaf", "blk"), None),
            P(None, ("leaf", "blk"), None),
            P(("leaf", "blk"), None),
            P(("leaf", "blk"), None),
            P(None, ("leaf", "blk"), None),
        ),
        out_specs=(P(("leaf", "blk"), None), P(None, ("leaf", "blk"), None)),
        check_vma=False,
    )
```

profile of v0, /device:TPU:1, one launch (start us, length us, event | category | flops | bytes accessed | tf_op | source)
XLA Modules:
  0.0 590.2 jit_solution(4690270651904076409)
XLA Ops:
  8.5 71.9 %all_to_all.10 = bf16[16,320,256]{2,1,0:T(8,128)(2,1)S(1)} all-to-all(bf16[16,320,256]{2,1,0:T(8,128)(2,1)S(1)} %broadcast_in_dim.4), channel_id=1, replica_groups=mesh['leaf'=16,'blk'=16] {'blk'}, dimensions={0} | all-to-all | bytes 5242880 | tf_op jit(solution)/shard_map/all_to_all | solution.py:15
  81.5 1.7 broadcast_in_dim.5
  83.2 3.8 all-to-all-start.1
  87.2 58.6 %all-to-all-done.1 = bf16[16,320,256]{2,1,0:T(8,128)(2,1)S(1)} async-done(((bf16[16,320,256]{2,1,0:T(8,128)(2,1)}), bf16[16,320,256]{2,1,0:T(8,128)(2,1)S(1)}, u32[]{:S(2)}, u32[]{:S(2)}) %all-to-all-start.1) | async-done | bytes 2621472 | tf_op jit(solution)/shard_map/all_to_all | solution.py:15
  145.9 1.8 convolution_negate_fusion
  149.6 2.6 collective-permute-done
  153.7 1.6 collective-permute-done.1
  156.0 41.3 %all-gather.8.cloned.1.call-done = bf16[2048,256]{1,0:T(8,128)(2,1)} async-done(((bf16[128,256]{1,0:T(8,128)(2,1)}), bf16[2048,256]{1,0:T(8,128)(2,1)}) %all-gather.8.cloned.1.call-update) | async-done | bytes 1048592 | tf_op jit(solution)/shard_map/all_gather | solution.py:43
  201.1 1.6 collective-permute-done.2
  203.5 38.2 %all-gather.10.cloned.1.call-done = bf16[2048,256]{1,0:T(8,128)(2,1)} async-done(((bf16[128,256]{1,0:T(8,128)(2,1)}), bf16[2048,256]{1,0:T(8,128)(2,1)}) %all-gather.10.cloned.1.call-update) | async-done | bytes 1048592 | tf_op jit(solution)/shard_map/all_gather | solution.py:43
  245.1 2.8 collective-permute-start.3
  247.9 2.8 collective-permute-done.3
  252.1 1.6 collective-permute-done.4
  253.7 2.8 collective-permute-start.5
  256.5 1.9 collective-permute-done.5
  259.2 41.3 %all-gather.12.cloned.1.call-done = bf16[4096,256]{1,0:T(8,128)(2,1)} async-done(((bf16[256,256]{1,0:T(8,128)(2,1)}), bf16[4096,256]{1,0:T(8,128)(2,1)}) %all-gather.12.cloned.1.call-update) | async-done | bytes 2097168 | tf_op jit(solution)/shard_map/all_gather | solution.py:43
  300.4 1.8 copy.28
  302.3 1.5 convolution_convert_fusion.3
  305.0 1.6 collective-permute-done.6
  306.7 2.8 collective-permute-start.7
  309.4 1.9 collective-permute-done.7
  312.1 40.2 %all-gather.14.cloned.1.call-done = bf16[4096,256]{1,0:T(8,128)(2,1)} async-done(((bf16[256,256]{1,0:T(8,128)(2,1)}), bf16[4096,256]{1,0:T(8,128)(2,1)}) %all-gather.14.cloned.1.call-update) | async-done | bytes 2097168 | tf_op jit(solution)/shard_map/all_gather | solution.py:43
  352.3 1.8 copy.29
  354.2 1.7 bitcast_subtract_fusion.1
  357.8 2.8 collective-permute-done.8
  362.2 1.6 collective-permute-done.9
  363.8 2.8 collective-permute-start.10
  366.6 1.9 collective-permute-done.10
  369.8 2.6 collective-permute-done.11
  373.3 44.7 %all-gather.16.cloned.1.call-done = bf16[8192,256]{1,0:T(8,128)(2,1)} async-done(((bf16[512,256]{1,0:T(8,128)(2,1)}), bf16[8192,256]{1,0:T(8,128)(2,1)}) %all-gather.16.cloned.1.call-update) | async-done | bytes 4194320 | tf_op jit(solution)/shard_map/all_gather | solution.py:43
  418.0 2.5 copy.33
  420.5 2.0 convolution_convert_fusion.1
  423.9 1.6 collective-permute-done.12
  425.5 2.8 collective-permute-start.13
  428.2 1.9 collective-permute-done.13
  431.5 2.6 collective-permute-done.14
  435.0 44.0 %all-gather.18.cloned.1.call-done = bf16[8192,256]{1,0:T(8,128)(2,1)} async-done(((bf16[512,256]{1,0:T(8,128)(2,1)}), bf16[8192,256]{1,0:T(8,128)(2,1)}) %all-gather.18.cloned.1.call-update) | async-done | bytes 4194320 | tf_op jit(solution)/shard_map/all_gather | solution.py:43
  479.0 2.7 copy.34
  483.5 2.8 collective-permute-start.15
  489.1 1.6 collective-permute-done.16
  490.8 2.8 collective-permute-start.17
  493.5 1.9 collective-permute-done.17
  496.8 2.6 collective-permute-done.18
  499.5 2.8 collective-permute-start.19
  502.3 5.4 collective-permute-done.19
  508.7 60.0 %all-gather.20.cloned.1.call-done = bf16[16384,256]{1,0:T(8,128)(2,1)} async-done(((bf16[1024,256]{1,0:T(8,128)(2,1)}), bf16[16384,256]{1,0:T(8,128)(2,1)}) %all-gather.20.cloned.1.call-update) | async-done | bytes 8388624 | tf_op jit(solution)/shard_map/all_gather | solution.py:43
  568.7 8.4 %copy.38 = bf16[16,16,64,256]{3,2,0,1:T(8,128)(2,1)} copy(bf16[16,16,64,256]{3,2,1,0:T(8,128)(2,1)} %bitcast.105) | data formatting | bytes 16777216 | tf_op jit(solution)/shard_map/reshape | solution.py:44
  577.1 5.6 fusion.10
  (114 shorter events, 35.6 us)
Async XLA Ops:
  7.2 73.2 %copy-start = (bf16[320,5120]{1,0:T(8,128)(2,1)S(1)}, bf16[320,5120]{1,0:T(8,128)(2,1)}, u32[]{:S(2)}) copy-start(bf16[320,5120]{1,0:T(8,128)(2,1)} %param.8) | copy-start | bytes 9830404
  81.4 1.7 copy-start.5
  83.2 3.8 copy-start.7
  83.2 62.7 %all-to-all-start.1 = ((bf16[16,320,256]{2,1,0:T(8,128)(2,1)}), bf16[16,320,256]{2,1,0:T(8,128)(2,1)S(1)}, u32[]{:S(2)}, u32[]{:S(2)}) async-start(bf16[16,320,256]{2,1,0:T(8,128)(2,1)} %broadcast_in_dim.5), calls=%async_computation.1 | async-start | bytes 5242880 | tf_op jit(solution)/shard_map/all_to_all | solution.py:15
  87.0 65.3 %slice-start.2 = ((bf16[4,64,256]{2,1,0:T(8,128)(2,1)}), bf16[1,64,256]{2,1,0:T(8,128)(2,1)S(1)}, s32[]{:S(2)}) async-start(bf16[4,64,256]{2,1,0:T(8,128)(2,1)} %param.10), calls=%async_computation.11 | async-start | bytes 65536 | tf_op jit(solution)/shard_map/slice | solution.py:75
  87.0 110.3 %all-gather.8.cloned.1.call-start = ((), (), s32[]{:S(2)}) async-start(), calls=%async_computation.2 | async-start | bytes 1114112 | tf_op jit(solution)/shard_map/all_gather | solution.py:43
  148.3 3.9 collective-permute-start
  152.4 2.9 collective-permute-start.1
  155.9 85.8 %all-gather.10.cloned.1.call-start = ((), (), s32[]{:S(2)}) async-start(), calls=%async_computation.3 | async-start | bytes 1114112 | tf_op jit(solution)/shard_map/all_gather | solution.py:43
  199.8 2.9 collective-permute-start.2
  203.4 97.1 %all-gather.12.cloned.1.call-start = ((), (), s32[]{:S(2)}) async-start(), calls=%async_computation.4 | async-start | bytes 2228224 | tf_op jit(solution)/shard_map/all_gather | solution.py:43
  203.5 47.3 %copy-start.6 = (bf16[4,64,256]{2,1,0:T(8,128)(2,1)S(1)}, bf16[4,64,256]{2,1,0:T(8,128)(2,1)}, u32[]{:S(2)}) copy-start(bf16[4,64,256]{2,1,0:T(8,128)(2,1)} %param.10) | copy-start | bytes 393220
  245.1 5.7 collective-permute-start.3
  250.8 61.3 %copy-start.4 = (f32[3,64,256]{2,1,0:T(8,128)}, f32[3,64,256]{2,1,0:T(8,128)S(1)}, u32[]{:S(2)}) copy-start(f32[3,64,256]{2,1,0:T(8,128)S(1)} %copy_add_fusion.1) | copy-start | bytes 589828
  250.8 2.9 collective-permute-start.4
  253.7 4.7 collective-permute-start.5
  259.1 93.2 %all-gather.14.cloned.1.call-start = ((), (), s32[]{:S(2)}) async-start(), calls=%async_computation.5 | async-start | bytes 2228224 | tf_op jit(solution)/shard_map/all_gather | solution.py:43
  303.8 2.9 collective-permute-start.6
  306.7 4.7 collective-permute-start.7
  312.1 106.0 %all-gather.16.cloned.1.call-start = ((), (), s32[]{:S(2)}) async-start(), calls=%async_computation.6 | async-start | bytes 4456448 | tf_op jit(solution)/shard_map/all_gather | solution.py:43
  312.1 42.0 %slice-start.1 = ((f32[3,64,256]{2,1,0:T(8,128)}), f32[2,64,256]{2,1,0:T(8,128)S(1)}, s32[]{:S(2)}) async-start(f32[3,64,256]{2,1,0:T(8,128)} %copy-done.4), calls=%async_computation.10 | async-start | bytes 262144 | tf_op jit(solution)/shard_map/slice | solution.py:92
  356.5 4.2 collective-permute-start.8
  360.7 74.3 %copy-start.3 = (f32[3,64,256]{2,1,0:T(8,128)}, f32[3,64,256]{2,1,0:T(8,128)S(1)}, u32[]{:S(2)}) copy-start(f32[3,64,256]{2,1,0:T(8,128)S(1)} %copy_add_fusion) | copy-start | bytes 589828
  360.7 3.0 collective-permute-start.9
  363.8 4.7 collective-permute-start.10
  368.5 3.9 collective-permute-start.11
  373.3 105.7 %all-gather.18.cloned.1.call-start = ((), (), s32[]{:S(2)}) async-start(), calls=%async_computation.7 | async-start | bytes 4456448 | tf_op jit(solution)/shard_map/all_gather | solution.py:43
  422.6 2.9 collective-permute-start.12
  425.5 4.7 collective-permute-start.13
  430.2 3.9 collective-permute-start.14
  434.9 133.8 %all-gather.20.cloned.1.call-start = ((), (), s32[]{:S(2)}) async-start(), calls=%async_computation.8 | async-start | bytes 8912896 | tf_op jit(solution)/shard_map/all_gather | solution.py:43
  479.0 3.3 copy-start.2
  479.0 3.3 slice-start
  483.5 4.4 collective-permute-start.15
  487.9 2.9 collective-permute-start.16
  490.8 4.7 collective-permute-start.17
  495.5 3.9 collective-permute-start.18
  499.5 8.2 %collective-permute-start.19 = (bf16[512,256]{1,0:T(8,128)(2,1)S(1)}, bf16[512,256]{1,0:T(8,128)(2,1)S(1)}, u32[]{:S(2)}, u32[]{:S(2)}) collective-permute-start(bf16[512,256]{1,0:T(8,128)(2,1)S(1)} %pad_maximum_fusion.3), channel_id=1, source_target_pairs={{0,128},{16,144},{32,160},{48,176},{64,192},{80,208},{96,224},{112... | collective-permute-start | bytes 786440 | tf_op jit(solution)/shard_map/ppermute | solution.py:10
  577.1 6.3 %copy-start.1 = (bf16[320,5120]{1,0:T(8,128)(2,1)S(1)}, bf16[320,5120]{1,0:T(8,128)(2,1)}, u32[]{:S(2)}) copy-start(bf16[320,5120]{1,0:T(8,128)(2,1)} %param.8) | copy-start | bytes 9830404
Sparse Core Ops, SparseCore 0:
  156.0 41.1 all-gather.7
  203.5 38.2 all-gather.9
  259.2 41.1 all-gather.11
  312.2 40.1 all-gather.13
  373.4 44.6 all-gather.15
  435.0 43.8 all-gather.17
  508.8 59.8 all-gather.19
where the time goes:
time: 591 us; the launch traced here: 590 us
  waiting for transfers between devices  412 us (70%)
  blocking collectives  71.9 us (12%)
  starting transfers between devices  42 us (7%)
  local copies, waits for them, and re-layouts  24.3 us (4%)
  matrix products  19 us (3%)
  between operations  14.7 us (2%)
  other arithmetic  6.32 us (1%)
    all_gather x7, waiting for transfers between devices, group_rows(): spread = lax.all_gather(joined, 'blk', axis=0, tiled=True)  310 us
    all_to_all x1, blocking collectives, from_everyone(): lax.all_to_all(jnp.broadcast_to(shard[None], (length, *shard.shape)), axi...  71.9 us
    all_to_all x1, waiting for transfers between devices, from_everyone(): lax.all_to_all(jnp.broadcast_to(shard[None], (length, *shard.shape)), axi...  58.6 us
    ppermute x20, waiting for transfers between devices, partner(): return lax.ppermute(value, axis, pairs)  43.5 us
    ppermute x20, starting transfers between devices, partner(): return lax.ppermute(value, axis, pairs)  38 us
    reshape x7, local copies, waits for them, and re-layouts, group_rows(): spread.reshape(lax.axis_size('blk'), 2 ** height, pieces.shape[0], pieces...  19.8 us
  transfers between devices with their start and end apart: 28, of which 28 were waited for; matrix products, arithmetic and copies ran while one was open for 0% of the time, Pallas kernels for 0%

commit v1 on v0

--- a/solution.py
+++ b/solution.py
@@ -40,7 +40,9 @@
     for bit_index in range(height):
         partner_rows = partner(joined, "leaf", bit_index)
         joined = pair_merge(joined, partner_rows, bit_index)
-    spread = lax.all_gather(joined, "blk", axis=0, tiled=True)
+    spread = jnp.concatenate(
+        lax.all_to_all(jnp.stack([joined] * lax.axis_size("blk")), "blk", 0, 0), axis=0
+    )
     spread = spread.reshape(lax.axis_size("blk"), 2**height, pieces.shape[0], pieces.shape[1])
     return jnp.transpose(spread, (1, 0, 2, 3)).reshape(-1, pieces.shape[1])
 

time: 591 us -> 843 us (1.43)
  blocking collectives: 71.9 us -> 467 us
  waiting for transfers between devices: 412 us -> 273 us
  starting transfers between devices: 42 us -> 57.5 us
  between operations: 14.7 us -> 1.25 us
    all_to_all x0 -> x4, blocking collectives: none -> 395 us  [group_rows(): lax.all_to_all(jnp.stack([joined] * lax.axis_size('blk')), 'blk', 0, 0)]
    all_gather x7 -> x0, waiting for transfers between devices: 310 us -> none  [group_rows(): spread = lax.all_gather(joined, 'blk', axis=0, tiled=True)]
    all_to_all x0 -> x3, waiting for transfers between devices: none -> 170 us  [group_rows(): lax.all_to_all(jnp.stack([joined] * lax.axis_size('blk')), 'blk', 0, 0)]
    reshape x7 -> x0, local copies, waits for them, and re-layouts: 19.8 us -> none  [group_rows(): spread.reshape(lax.axis_size('blk'), 2 ** height, pieces.shape[0], pieces...]
    all_to_all x0 -> x3, starting transfers between devices: none -> 14.8 us  [group_rows(): lax.all_to_all(jnp.stack([joined] * lax.axis_size('blk')), 'blk', 0, 0)]
    transpose x0 -> x7, local copies, waits for them, and re-layouts: none -> 12 us  [group_rows(): return jnp.transpose(spread, (1, 0, 2, 3)).reshape(-1, pieces.shape[1])]
  transfers between devices with their start and end apart: 28 -> 24, of which waited for: 28 -> 24; matrix products, arithmetic and copies ran while one was open for 0% -> 0% of each run, Pallas kernels for 0% -> 0%
where the time goes in v1:
time: 843 us
  blocking collectives  467 us (55%)
  waiting for transfers between devices  273 us (32%)
  starting transfers between devices  57.5 us (7%)
  local copies, waits for them, and re-layouts  23.1 us (3%)
  matrix products  19 us (2%)
    all_to_all x4, blocking collectives, group_rows(): lax.all_to_all(jnp.stack([joined] * lax.axis_size('blk')), 'blk', 0, 0)  395 us
    all_to_all x3, waiting for transfers between devices, group_rows(): lax.all_to_all(jnp.stack([joined] * lax.axis_size('blk')), 'blk', 0, 0)  170 us
    all_to_all x1, blocking collectives, from_everyone(): lax.all_to_all(jnp.broadcast_to(shard[None], (length, *shard.shape)), axi...  71.9 us
    all_to_all x1, waiting for transfers between devices, from_everyone(): lax.all_to_all(jnp.broadcast_to(shard[None], (length, *shard.shape)), axi...  58.7 us
    ppermute x20, waiting for transfers between devices, partner(): return lax.ppermute(value, axis, pairs)  43.6 us
    ppermute x20, starting transfers between devices, partner(): return lax.ppermute(value, axis, pairs)  39.1 us
  transfers between devices with their start and end apart: 24, of which 24 were waited for; matrix products, arithmetic and copies ran while one was open for 0% of the time, Pallas kernels for 0%

profile of v1, /device:TPU:1, one launch (start us, length us, event | category | flops | bytes accessed | tf_op | source)
XLA Modules:
  0.0 842.5 jit_solution(5193098779468351939)
XLA Ops:
  2.0 71.9 %all_to_all.45 = bf16[16,320,256]{2,1,0:T(8,128)(2,1)S(1)} all-to-all(bf16[16,320,256]{2,1,0:T(8,128)(2,1)S(1)} %broadcast_in_dim.4), channel_id=1, replica_groups=mesh['leaf'=16,'blk'=16] {'blk'}, dimensions={0} | all-to-all | bytes 5242880 | tf_op jit(solution)/shard_map/all_to_all | solution.py:15
  74.9 1.7 broadcast_in_dim.5
  76.7 3.6 all-to-all-start.1
  80.6 58.7 %all-to-all-done.1 = bf16[16,320,256]{2,1,0:T(8,128)(2,1)S(1)} async-done(((bf16[16,320,256]{2,1,0:T(8,128)(2,1)}), bf16[16,320,256]{2,1,0:T(8,128)(2,1)S(1)}, u32[]{:S(2)}, u32[]{:S(2)}) %all-to-all-start.1) | async-done | bytes 2621472 | tf_op jit(solution)/shard_map/all_to_all | solution.py:15
  139.2 1.8 convolution_negate_fusion
  143.0 2.6 collective-permute-done
  147.0 1.6 collective-permute-done.1
  148.7 36.7 %all_to_all.46 = bf16[16,128,256]{2,1,0:T(8,128)(2,1)S(1)} all-to-all(bf16[16,128,256]{2,1,0:T(8,128)(2,1)S(1)} %stack.24), channel_id=1, replica_groups=mesh['leaf'=16,'blk'=16] {'blk'}, dimensions={0} | all-to-all | bytes 2097152 | tf_op jit(solution)/shard_map/all_to_all | solution.py:44
  188.0 1.6 collective-permute-done.2
  190.7 4.1 all-to-all-start.3
  195.0 27.9 %all-to-all-done.3 = bf16[16,128,256]{2,1,0:T(8,128)(2,1)S(1)} async-done(((bf16[16,128,256]{2,1,0:T(8,128)(2,1)}), bf16[16,128,256]{2,1,0:T(8,128)(2,1)S(1)}, u32[]{:S(2)}, u32[]{:S(2)}) %all-to-all-start.3) | async-done | bytes 1048608 | tf_op jit(solution)/shard_map/all_to_all | solution.py:44
  225.0 2.8 collective-permute-start.3
  227.8 2.3 collective-permute-done.3
  231.5 2.0 collective-permute-done.4
  233.5 2.8 collective-permute-start.5
  236.4 1.9 collective-permute-done.5
  238.5 57.2 %all_to_all.47 = bf16[16,256,256]{2,1,0:T(8,128)(2,1)S(1)} all-to-all(bf16[16,256,256]{2,1,0:T(8,128)(2,1)S(1)} %stack.27), channel_id=1, replica_groups=mesh['leaf'=16,'blk'=16] {'blk'}, dimensions={0} | all-to-all | bytes 4194304 | tf_op jit(solution)/shard_map/all_to_all | solution.py:44
  298.7 1.6 collective-permute-done.6
  300.3 2.8 collective-permute-start.7
  303.1 2.4 collective-permute-done.7
  307.1 4.7 all-to-all-start.5
  311.9 49.0 %all-to-all-done.5 = bf16[16,256,256]{2,1,0:T(8,128)(2,1)S(1)} async-done(((bf16[16,256,256]{2,1,0:T(8,128)(2,1)}), bf16[16,256,256]{2,1,0:T(8,128)(2,1)S(1)}, u32[]{:S(2)}, u32[]{:S(2)}) %all-to-all-start.5) | async-done | bytes 2097184 | tf_op jit(solution)/shard_map/all_to_all | solution.py:44
  361.0 1.7 bitcast_subtract_fusion.1
  363.4 1.6 collective-permute-start.8
  365.0 2.7 collective-permute-done.8
  370.7 2.8 collective-permute-start.10
  373.5 1.9 collective-permute-done.10
  376.8 2.5 collective-permute-done.11
  379.8 104.7 %all_to_all.48 = bf16[16,512,256]{2,1,0:T(8,128)(2,1)S(1)} all-to-all(bf16[16,512,256]{2,1,0:T(8,128)(2,1)S(1)} %stack.30), channel_id=1, replica_groups=mesh['leaf'=16,'blk'=16] {'blk'}, dimensions={0} | all-to-all | bytes 8388608 | tf_op jit(solution)/shard_map/all_to_all | solution.py:44
  485.1 2.0 convolution_convert_fusion.1
  488.4 1.6 collective-permute-done.12
  490.0 2.8 collective-permute-start.13
  492.8 2.4 collective-permute-done.13
  496.7 2.9 collective-permute-done.14
  499.7 2.4 stack.32
  502.1 6.0 all-to-all-start.7
  508.1 93.6 %all-to-all-done.7 = bf16[16,512,256]{2,1,0:T(8,128)(2,1)} async-done(((bf16[16,512,256]{2,1,0:T(8,128)(2,1)}), bf16[16,512,256]{2,1,0:T(8,128)(2,1)}, u32[]{:S(2)}, u32[]{:S(2)}) %all-to-all-start.7) | async-done | bytes 4194336 | tf_op jit(solution)/shard_map/all_to_all | solution.py:44
  601.7 2.7 copy.46
  606.2 3.0 collective-permute-start.15
  611.9 1.6 collective-permute-done.16
  613.5 2.8 collective-permute-start.17
  616.3 1.9 collective-permute-done.17
  619.6 2.6 collective-permute-done.18
  622.3 3.0 collective-permute-start.19
  625.3 4.9 collective-permute-done.19
  631.1 196.8 %all_to_all.49 = bf16[16,1024,256]{2,1,0:T(8,128)(2,1)} all-to-all(bf16[16,1024,256]{2,1,0:T(8,128)(2,1)S(1)} %stack.33), channel_id=1, replica_groups=mesh['leaf'=16,'blk'=16] {'blk'}, dimensions={0} | all-to-all | bytes 16777216 | tf_op jit(solution)/shard_map/all_to_all | solution.py:44
  827.9 8.3 copy.50
  836.2 5.6 fusion.10
  (110 shorter events, 34.7 us)
Async XLA Ops:
  0.6 73.2 %copy-start = (bf16[320,5120]{1,0:T(8,128)(2,1)S(1)}, bf16[320,5120]{1,0:T(8,128)(2,1)}, u32[]{:S(2)}) copy-start(bf16[320,5120]{1,0:T(8,128)(2,1)} %param.8) | copy-start | bytes 9830404
  74.9 1.8 copy-start.5
  74.9 5.4 copy-start.7
  76.7 62.5 %all-to-all-start.1 = ((bf16[16,320,256]{2,1,0:T(8,128)(2,1)}), bf16[16,320,256]{2,1,0:T(8,128)(2,1)S(1)}, u32[]{:S(2)}, u32[]{:S(2)}) async-start(bf16[16,320,256]{2,1,0:T(8,128)(2,1)} %broadcast_in_dim.5), calls=%async_computation.1 | async-start | bytes 5242880 | tf_op jit(solution)/shard_map/all_to_all | solution.py:15
  80.3 65.3 %slice-start.2 = ((bf16[4,64,256]{2,1,0:T(8,128)(2,1)}), bf16[1,64,256]{2,1,0:T(8,128)(2,1)S(1)}, s32[]{:S(2)}) async-start(bf16[4,64,256]{2,1,0:T(8,128)(2,1)} %param.10), calls=%async_computation.11 | async-start | bytes 65536 | tf_op jit(solution)/shard_map/slice | solution.py:77
  141.7 3.9 collective-permute-start
  145.7 2.9 collective-permute-start.1
  186.7 2.9 collective-permute-start.2
  190.7 32.1 %all-to-all-start.3 = ((bf16[16,128,256]{2,1,0:T(8,128)(2,1)}), bf16[16,128,256]{2,1,0:T(8,128)(2,1)S(1)}, u32[]{:S(2)}, u32[]{:S(2)}) async-start(bf16[16,128,256]{2,1,0:T(8,128)(2,1)} %stack.26), calls=%async_computation.3 | async-start | bytes 2097152 | tf_op jit(solution)/shard_map/all_to_all | solution.py:44
  194.9 35.3 %copy-start.6 = (bf16[4,64,256]{2,1,0:T(8,128)(2,1)S(1)}, bf16[4,64,256]{2,1,0:T(8,128)(2,1)}, u32[]{:S(2)}) copy-start(bf16[4,64,256]{2,1,0:T(8,128)(2,1)} %param.10) | copy-start | bytes 393220
  225.0 5.2 collective-permute-start.3
  230.2 81.7 %copy-start.4 = (f32[3,64,256]{2,1,0:T(8,128)}, f32[3,64,256]{2,1,0:T(8,128)S(1)}, u32[]{:S(2)}) copy-start(f32[3,64,256]{2,1,0:T(8,128)S(1)} %copy_add_fusion.1) | copy-start | bytes 589828
  230.2 3.3 collective-permute-start.4
  233.5 4.7 collective-permute-start.5
  297.4 2.9 collective-permute-start.6
  300.3 5.3 collective-permute-start.7
  307.1 53.8 %all-to-all-start.5 = ((bf16[16,256,256]{2,1,0:T(8,128)(2,1)}), bf16[16,256,256]{2,1,0:T(8,128)(2,1)S(1)}, u32[]{:S(2)}, u32[]{:S(2)}) async-start(bf16[16,256,256]{2,1,0:T(8,128)(2,1)} %stack.29), calls=%async_computation.5 | async-start | bytes 4194304 | tf_op jit(solution)/shard_map/all_to_all | solution.py:44
  311.9 49.2 %slice-start.1 = ((f32[3,64,256]{2,1,0:T(8,128)}), f32[2,64,256]{2,1,0:T(8,128)S(1)}, s32[]{:S(2)}) async-start(f32[3,64,256]{2,1,0:T(8,128)} %copy-done.4), calls=%async_computation.10 | async-start | bytes 262144 | tf_op jit(solution)/shard_map/slice | solution.py:94
  363.4 4.3 collective-permute-start.8
  367.8 140.4 %copy-start.3 = (f32[3,64,256]{2,1,0:T(8,128)}, f32[3,64,256]{2,1,0:T(8,128)S(1)}, u32[]{:S(2)}) copy-start(f32[3,64,256]{2,1,0:T(8,128)S(1)} %copy_add_fusion) | copy-start | bytes 589828
  367.8 2.9 collective-permute-start.9
  370.7 4.7 collective-permute-start.10
  375.4 3.9 collective-permute-start.11
  487.1 2.9 collective-permute-start.12
  490.0 5.3 collective-permute-start.13
  495.3 4.3 collective-permute-start.14
  502.1 99.5 %all-to-all-start.7 = ((bf16[16,512,256]{2,1,0:T(8,128)(2,1)}), bf16[16,512,256]{2,1,0:T(8,128)(2,1)}, u32[]{:S(2)}, u32[]{:S(2)}) async-start(bf16[16,512,256]{2,1,0:T(8,128)(2,1)} %stack.32), calls=%async_computation.7 | async-start | bytes 8388608 | tf_op jit(solution)/shard_map/all_to_all | solution.py:44
  601.7 3.3 copy-start.2
  601.7 3.3 slice-start
  606.2 4.4 collective-permute-start.15
  610.6 2.9 collective-permute-start.16
  613.5 4.7 collective-permute-start.17
  618.2 4.0 collective-permute-start.18
  622.3 7.9 collective-permute-start.19
  836.2 6.3 copy-start.1
